TPU v7x, 32 devices: a whole 2x2x4 slice. The times are simulated.
32 devices in a mesh: section: 4 (over y, x), expert: 8 (over z, core).
Axes of the slice: x: 2, y: 2, z: 4, core: 2. Of those that a mesh axis runs over, the one named last changes fastest.
Arguments:
- tokens: bfloat16 [8, 64, 2048], P(None, 'expert'), may hold values from -6 to 6
- norm_gain: float32 [2, 2048], replicated, may hold values from 0.1 to 1.9
- w_gate: bfloat16 [4, 2048, 14336], P('section', None, 'expert'), may hold values from -0.125 to 0.125
- w_up: bfloat16 [4, 2048, 14336], P('section', None, 'expert'), may hold values from -0.125 to 0.125
- w_down: bfloat16 [4, 14336, 2048], P('section', 'expert'), may hold values from -0.0625 to 0.0625
- expert_ids: int32 [2, 8, 64, 2], P(None, None, 'expert'), may hold values from 0 to 3, as said below
- slot_ids: int32 [2, 8, 64, 2], P(None, None, 'expert'), may hold values from 0 to 4, as said below
- dropped: int32 [2, 8, 64, 2], P(None, None, 'expert'), may hold values from 0 to 1, as said below
- gate_weights: float32 [2, 8, 64, 2], P(None, None, 'expert'), may hold values from 0.1 to 1
Outputs:
- states: bfloat16 [4, 8, 64, 2048], P('section', None, 'expert')
Inputs may be any that keep to these rules, and one draw needn't show every extreme that they name: `expert_ids`: the two experts of a token differ. `slot_ids`: among the kept choices of the tokens of one index of expert that name one expert, the slots are 0, 1, ... up to their count less one, each once. At most 5 kept choices of the tokens of one index of expert name one expert, and a choice is dropped only where 5 kept choices of its index of expert name its expert; in each layer and micro-batch some expert receives exactly 5 kept choices from every index of expert.
All inputs are finite; a program needn't handle non-finite values.
Results may differ from a plain program's by a relative error of at most 0.025.
Values may be sent and summed in bfloat16 or wider, within the bound.
A program may use at most 64 MiB of HBM per device.

v0:
```python
import jax
import jax.numpy as jnp
from jax import lax
from jax.sharding import PartitionSpec as P

EXPERTS = 4


def shortened(value):
    return jax.tree.map(lambda a: a.astype(jnp.bfloat16) if a.dtype == jnp.float32 else a, value)


def shifted(value, axis, by):
    size = lax.axis_size(axis)
    pairs = [(i, i + by) for i in range(size) if 0 <= i + by < size]
    return lax.ppermute(value, axis, pairs)


def on_device(tokens, norm_gain, w_gate, w_up, w_down, expert_ids, slot_ids, dropped, gate_weights):
    groups = lax.axis_size("expert")
    sections = lax.axis_size("section")
    section_at = lax.axis_index("section")
    local_count = EXPERTS // 2
    shards = groups // local_count
    micro_count, tok_rows, model_width = tokens.shape
    capacity = 5 * tok_rows // (2 * EXPERTS)
    slot_limit = local_count * capacity
    layer_at = section_at // 2
    half_at = section_at % 2
    odd_section = half_at == 1
    gain_row = lax.dynamic_index_in_dim(norm_gain, layer_at, 0, keepdims=False)
    gate_mat = w_gate[0]
    up_mat = w_up[0]
    down_mat = w_down[0]
    route_all = lax.dynamic_index_in_dim(expert_ids, layer_at, 0, keepdims=False)
    slot_all = lax.dynamic_index_in_dim(slot_ids, layer_at, 0, keepdims=False)
    drop_all = lax.dynamic_index_in_dim(dropped, layer_at, 0, keepdims=False)
    weigh_all = lax.dynamic_index_in_dim(gate_weights, layer_at, 0, keepdims=False)

    def expert_rows(received):
        flat_rows = received.reshape(-1, model_width)
        gate_vals = jnp.dot(flat_rows, gate_mat, preferred_element_type=jnp.float32)
        up_vals = jnp.dot(flat_rows, up_mat, preferred_element_type=jnp.float32)
        hidden = (jax.nn.silu(gate_vals) * up_vals).astype(jnp.bfloat16)
        partial_rows = jnp.dot(hidden, down_mat, preferred_element_type=jnp.float32).astype(
            jnp.bfloat16
        )
        return partial_rows.reshape(received.shape)

    def skip_rows(received):
        return jnp.zeros(received.shape, jnp.bfloat16)

    def run_experts(outgoing, active):
        received = lax.all_to_all(outgoing, "expert", split_axis=0, concat_axis=0, tiled=True)
        computed = lax.cond(active, expert_rows, skip_rows, received)
        returned = lax.all_to_all(computed, "expert", split_axis=0, concat_axis=0, tiled=True)
        return returned

    def advance(tick_count, carry):
        incoming, states = carry
        micro_at = tick_count - section_at
        active = (micro_at >= 0) & (micro_at < micro_count)
        micro_index = jnp.clip(micro_at, 0, micro_count - 1)
        fresh_rows = lax.dynamic_index_in_dim(tokens, micro_index, 0, keepdims=False)
        route_now = lax.dynamic_index_in_dim(route_all, micro_index, 0, keepdims=False)
        slot_now = lax.dynamic_index_in_dim(slot_all, micro_index, 0, keepdims=False)
        drop_now = lax.dynamic_index_in_dim(drop_all, micro_index, 0, keepdims=False)
        weigh_now = lax.dynamic_index_in_dim(weigh_all, micro_index, 0, keepdims=False)
        kept_mask = drop_now == 0
        passed_state = incoming[0]
        prior_rows = [incoming[1], incoming[2]]
        current = jnp.where(section_at == 0, fresh_rows, passed_state)
        wide_rows = current.astype(jnp.float32)
        inv_scale = lax.rsqrt(jnp.mean(wide_rows * wide_rows, axis=-1, keepdims=True) + 1e-05)
        normed = (wide_rows * inv_scale * gain_row).astype(jnp.bfloat16)
        local_id = route_now - half_at * local_count
        owned = kept_mask & (local_id >= 0) & (local_id < local_count)
        target = jnp.where(owned, local_id * capacity + slot_now, slot_limit)
        buffer = jnp.zeros((slot_limit, model_width), jnp.bfloat16)
        buffer = buffer.at[target[:, 0]].set(normed, mode="drop")
        buffer = buffer.at[target[:, 1]].set(normed, mode="drop")
        buffer = buffer.reshape(local_count, capacity, model_width)
        outgoing = jnp.repeat(buffer, shards, axis=0)
        returned = run_experts(outgoing, active)
        summed = jnp.sum(
            returned.astype(jnp.float32).reshape(local_count, shards, capacity, model_width), axis=1
        )
        flat_back = summed.astype(jnp.bfloat16).reshape(slot_limit, model_width)
        clipped = jnp.minimum(target, slot_limit - 1)
        combined = wide_rows
        chosen_rows = []
        for member in range(2):
            own_rows = flat_back[clipped[:, member]]
            chosen = jnp.where(owned[:, member : member + 1], own_rows, prior_rows[member])
            chosen_rows.append(chosen)
            combined = combined + weigh_now[:, member : member + 1] * chosen.astype(jnp.float32)
        mixed_rows = combined.astype(jnp.bfloat16)
        updated = lax.dynamic_update_index_in_dim(states, mixed_rows, micro_index, 0)
        states = jnp.where(active, updated, states)
        zero_rows = jnp.zeros_like(current)
        even_load = jnp.stack([current, chosen_rows[0], chosen_rows[1]])
        odd_load = jnp.stack([mixed_rows, zero_rows, zero_rows])
        payload = jnp.where(odd_section, odd_load, even_load)
        passed = shifted(shortened(payload), "section", 1).astype(payload.dtype)
        return (passed, states)

    start_load = jnp.zeros((3, tok_rows, model_width), jnp.bfloat16)
    initial = (start_load, jnp.zeros((micro_count, tok_rows, model_width), jnp.bfloat16))
    final_load, states = lax.fori_loop(0, micro_count + sections - 1, advance, initial)
    return states[None]


def solution(mesh):
    return jax.shard_map(
        on_device,
        mesh=mesh,
        in_specs=(
            P(None, "expert", None),
            P(),
            P("section", None, "expert"),
            P("section", None, "expert"),
            P("section", "expert", None),
            P(None, None, "expert", None),
            P(None, None, "expert", None),
            P(None, None, "expert", None),
            P(None, None, "expert", None),
        ),
        out_specs=P("section", None, "expert", None),
        check_vma=False,
    )
```

profile of v0, /device:TPU:6, one launch (start us, length us, event | category | flops | bytes accessed | tf_op | source)
XLA Modules:
  0.0 560.5 jit_solution(8104722328637122049)
XLA Ops:
  2.2 557.6 %while.17 = (s32[]{:T(128)}, bf16[3,8,2048]{2,1,0:T(8,128)(2,1)S(1)}, bf16[8,8,2048]{2,1,0:T(8,128)(2,1)S(1)}, pred[]{:T(512)}, pred[]{:T(512)}, /*index=5*/s32[...) while((s32[]{:T(128)}, ...), condition=%wide.region_7.8_spmd, body=%wide.region_0.7_spmd.sunk | while | flops 881903936 | bytes 27046772 | solution.py:109
  10.4 9.7 %all-to-all-done = bf16[8,5,2048]{2,1,0:T(8,128)(2,1)S(1)} async-done(((bf16[8,5,2048]{2,1,0:T(8,128)(2,1)}), bf16[8,5,2048]{2,1,0:T(8,128)(2,1)S(1)}, u32[]{:S(2)}, u32[]{:S(2)}) %all-to-all-start) | async-done | bytes 163872 | tf_op jit(solution)/shard_map/while/body/eval_jaxpr/all_to_all | solution.py:54
  24.3 9.6 %all-to-all-done.1 = bf16[8,5,2048]{2,1,0:T(8,128)(2,1)S(1)} async-done(((bf16[8,5,2048]{2,1,0:T(8,128)(2,1)}), bf16[8,5,2048]{2,1,0:T(8,128)(2,1)S(1)}, u32[]{:S(2)}, u32[]{:S(2)}) %all-to-all-start.1) | async-done | bytes 163872 | tf_op jit(solution)/shard_map/while/body/eval_jaxpr/all_to_all | solution.py:56
  48.5 9.6 %all-to-all-done = bf16[8,5,2048]{2,1,0:T(8,128)(2,1)S(1)} async-done(((bf16[8,5,2048]{2,1,0:T(8,128)(2,1)}), bf16[8,5,2048]{2,1,0:T(8,128)(2,1)S(1)}, u32[]{:S(2)}, u32[]{:S(2)}) %all-to-all-start) | async-done | bytes 163872 | tf_op jit(solution)/shard_map/while/body/eval_jaxpr/all_to_all | solution.py:54
  62.3 9.6 %all-to-all-done.1 = bf16[8,5,2048]{2,1,0:T(8,128)(2,1)S(1)} async-done(((bf16[8,5,2048]{2,1,0:T(8,128)(2,1)}), bf16[8,5,2048]{2,1,0:T(8,128)(2,1)S(1)}, u32[]{:S(2)}, u32[]{:S(2)}) %all-to-all-start.1) | async-done | bytes 163872 | tf_op jit(solution)/shard_map/while/body/eval_jaxpr/all_to_all | solution.py:56
  86.5 9.6 %all-to-all-done = bf16[8,5,2048]{2,1,0:T(8,128)(2,1)S(1)} async-done(((bf16[8,5,2048]{2,1,0:T(8,128)(2,1)}), bf16[8,5,2048]{2,1,0:T(8,128)(2,1)S(1)}, u32[]{:S(2)}, u32[]{:S(2)}) %all-to-all-start) | async-done | bytes 163872 | tf_op jit(solution)/shard_map/while/body/eval_jaxpr/all_to_all | solution.py:54
  100.3 9.6 %all-to-all-done.1 = bf16[8,5,2048]{2,1,0:T(8,128)(2,1)S(1)} async-done(((bf16[8,5,2048]{2,1,0:T(8,128)(2,1)}), bf16[8,5,2048]{2,1,0:T(8,128)(2,1)S(1)}, u32[]{:S(2)}, u32[]{:S(2)}) %all-to-all-start.1) | async-done | bytes 163872 | tf_op jit(solution)/shard_map/while/body/eval_jaxpr/all_to_all | solution.py:56
  112.6 38.1 %collective-permute-done = bf16[3,8,2048]{2,1,0:T(8,128)(2,1)S(1)} collective-permute-done((bf16[3,8,2048]{2,1,0:T(8,128)(2,1)S(1)}, bf16[3,8,2048]{2,1,0:T(8,128)(2,1)S(1)}, u32[]{:S(2)}, u32[]{:S(2)}) %collective-permute-start) | collective-permute-done | bytes 98336 | tf_op jit(solution)/shard_map/while/body/eval_jaxpr/ppermute | solution.py:16
  157.4 9.6 %all-to-all-done = bf16[8,5,2048]{2,1,0:T(8,128)(2,1)S(1)} async-done(((bf16[8,5,2048]{2,1,0:T(8,128)(2,1)}), bf16[8,5,2048]{2,1,0:T(8,128)(2,1)S(1)}, u32[]{:S(2)}, u32[]{:S(2)}) %all-to-all-start) | async-done | bytes 163872 | tf_op jit(solution)/shard_map/while/body/eval_jaxpr/all_to_all | solution.py:54
  167.0 13.1 %conditional.2 = (bf16[8,5,2048]{2,1,0:T(8,128)(2,1)}) conditional(s32[]{:T(128)} %convert_element_type.138, () %tuple.73, (bf16[8,5,2048]{2,1,0:T(8,128)(2,1)S(1)}, bf16[2048,1792]{1,0:T(8,128)(2,1)}, bf16[2048,1792]{1,0:T(8,128)(2,1)}, bf16[1792,2048]{1,0:T(8,128)(2,1)}) %tuple.74), branch_computations={%region_4.4_spmd, %region_5.5_spmd} | conditional | flops 881315840 | bytes 23740424 | solution.py:55
  183.5 9.6 %all-to-all-done.1 = bf16[8,5,2048]{2,1,0:T(8,128)(2,1)S(1)} async-done(((bf16[8,5,2048]{2,1,0:T(8,128)(2,1)}), bf16[8,5,2048]{2,1,0:T(8,128)(2,1)S(1)}, u32[]{:S(2)}, u32[]{:S(2)}) %all-to-all-start.1) | async-done | bytes 163872 | tf_op jit(solution)/shard_map/while/body/eval_jaxpr/all_to_all | solution.py:56
  208.7 9.6 %all-to-all-done = bf16[8,5,2048]{2,1,0:T(8,128)(2,1)S(1)} async-done(((bf16[8,5,2048]{2,1,0:T(8,128)(2,1)}), bf16[8,5,2048]{2,1,0:T(8,128)(2,1)S(1)}, u32[]{:S(2)}, u32[]{:S(2)}) %all-to-all-start) | async-done | bytes 163872 | tf_op jit(solution)/shard_map/while/body/eval_jaxpr/all_to_all | solution.py:54
  218.3 13.1 %conditional.2 = (bf16[8,5,2048]{2,1,0:T(8,128)(2,1)}) conditional(s32[]{:T(128)} %convert_element_type.138, () %tuple.73, (bf16[8,5,2048]{2,1,0:T(8,128)(2,1)S(1)}, bf16[2048,1792]{1,0:T(8,128)(2,1)}, bf16[2048,1792]{1,0:T(8,128)(2,1)}, bf16[1792,2048]{1,0:T(8,128)(2,1)}) %tuple.74), branch_computations={%region_4.4_spmd, %region_5.5_spmd} | conditional | flops 881315840 | bytes 23740424 | solution.py:55
  234.8 9.6 %all-to-all-done.1 = bf16[8,5,2048]{2,1,0:T(8,128)(2,1)S(1)} async-done(((bf16[8,5,2048]{2,1,0:T(8,128)(2,1)}), bf16[8,5,2048]{2,1,0:T(8,128)(2,1)S(1)}, u32[]{:S(2)}, u32[]{:S(2)}) %all-to-all-start.1) | async-done | bytes 163872 | tf_op jit(solution)/shard_map/while/body/eval_jaxpr/all_to_all | solution.py:56
  259.9 9.6 %all-to-all-done = bf16[8,5,2048]{2,1,0:T(8,128)(2,1)S(1)} async-done(((bf16[8,5,2048]{2,1,0:T(8,128)(2,1)}), bf16[8,5,2048]{2,1,0:T(8,128)(2,1)S(1)}, u32[]{:S(2)}, u32[]{:S(2)}) %all-to-all-start) | async-done | bytes 163872 | tf_op jit(solution)/shard_map/while/body/eval_jaxpr/all_to_all | solution.py:54
  269.5 13.1 %conditional.2 = (bf16[8,5,2048]{2,1,0:T(8,128)(2,1)}) conditional(s32[]{:T(128)} %convert_element_type.138, () %tuple.73, (bf16[8,5,2048]{2,1,0:T(8,128)(2,1)S(1)}, bf16[2048,1792]{1,0:T(8,128)(2,1)}, bf16[2048,1792]{1,0:T(8,128)(2,1)}, bf16[1792,2048]{1,0:T(8,128)(2,1)}) %tuple.74), branch_computations={%region_4.4_spmd, %region_5.5_spmd} | conditional | flops 881315840 | bytes 23740424 | solution.py:55
  286.1 9.6 %all-to-all-done.1 = bf16[8,5,2048]{2,1,0:T(8,128)(2,1)S(1)} async-done(((bf16[8,5,2048]{2,1,0:T(8,128)(2,1)}), bf16[8,5,2048]{2,1,0:T(8,128)(2,1)S(1)}, u32[]{:S(2)}, u32[]{:S(2)}) %all-to-all-start.1) | async-done | bytes 163872 | tf_op jit(solution)/shard_map/while/body/eval_jaxpr/all_to_all | solution.py:56
  311.2 9.6 %all-to-all-done = bf16[8,5,2048]{2,1,0:T(8,128)(2,1)S(1)} async-done(((bf16[8,5,2048]{2,1,0:T(8,128)(2,1)}), bf16[8,5,2048]{2,1,0:T(8,128)(2,1)S(1)}, u32[]{:S(2)}, u32[]{:S(2)}) %all-to-all-start) | async-done | bytes 163872 | tf_op jit(solution)/shard_map/while/body/eval_jaxpr/all_to_all | solution.py:54
  320.8 13.1 %conditional.2 = (bf16[8,5,2048]{2,1,0:T(8,128)(2,1)}) conditional(s32[]{:T(128)} %convert_element_type.138, () %tuple.73, (bf16[8,5,2048]{2,1,0:T(8,128)(2,1)S(1)}, bf16[2048,1792]{1,0:T(8,128)(2,1)}, bf16[2048,1792]{1,0:T(8,128)(2,1)}, bf16[1792,2048]{1,0:T(8,128)(2,1)}) %tuple.74), branch_computations={%region_4.4_spmd, %region_5.5_spmd} | conditional | flops 881315840 | bytes 23740424 | solution.py:55
  337.3 9.6 %all-to-all-done.1 = bf16[8,5,2048]{2,1,0:T(8,128)(2,1)S(1)} async-done(((bf16[8,5,2048]{2,1,0:T(8,128)(2,1)}), bf16[8,5,2048]{2,1,0:T(8,128)(2,1)S(1)}, u32[]{:S(2)}, u32[]{:S(2)}) %all-to-all-start.1) | async-done | bytes 163872 | tf_op jit(solution)/shard_map/while/body/eval_jaxpr/all_to_all | solution.py:56
  362.5 9.6 %all-to-all-done = bf16[8,5,2048]{2,1,0:T(8,128)(2,1)S(1)} async-done(((bf16[8,5,2048]{2,1,0:T(8,128)(2,1)}), bf16[8,5,2048]{2,1,0:T(8,128)(2,1)S(1)}, u32[]{:S(2)}, u32[]{:S(2)}) %all-to-all-start) | async-done | bytes 163872 | tf_op jit(solution)/shard_map/while/body/eval_jaxpr/all_to_all | solution.py:54
  372.0 13.1 %conditional.2 = (bf16[8,5,2048]{2,1,0:T(8,128)(2,1)}) conditional(s32[]{:T(128)} %convert_element_type.138, () %tuple.73, (bf16[8,5,2048]{2,1,0:T(8,128)(2,1)S(1)}, bf16[2048,1792]{1,0:T(8,128)(2,1)}, bf16[2048,1792]{1,0:T(8,128)(2,1)}, bf16[1792,2048]{1,0:T(8,128)(2,1)}) %tuple.74), branch_computations={%region_4.4_spmd, %region_5.5_spmd} | conditional | flops 881315840 | bytes 23740424 | solution.py:55
  388.6 9.6 %all-to-all-done.1 = bf16[8,5,2048]{2,1,0:T(8,128)(2,1)S(1)} async-done(((bf16[8,5,2048]{2,1,0:T(8,128)(2,1)}), bf16[8,5,2048]{2,1,0:T(8,128)(2,1)S(1)}, u32[]{:S(2)}, u32[]{:S(2)}) %all-to-all-start.1) | async-done | bytes 163872 | tf_op jit(solution)/shard_map/while/body/eval_jaxpr/all_to_all | solution.py:56
  413.7 9.6 %all-to-all-done = bf16[8,5,2048]{2,1,0:T(8,128)(2,1)S(1)} async-done(((bf16[8,5,2048]{2,1,0:T(8,128)(2,1)}), bf16[8,5,2048]{2,1,0:T(8,128)(2,1)S(1)}, u32[]{:S(2)}, u32[]{:S(2)}) %all-to-all-start) | async-done | bytes 163872 | tf_op jit(solution)/shard_map/while/body/eval_jaxpr/all_to_all | solution.py:54
  423.3 13.1 %conditional.2 = (bf16[8,5,2048]{2,1,0:T(8,128)(2,1)}) conditional(s32[]{:T(128)} %convert_element_type.138, () %tuple.73, (bf16[8,5,2048]{2,1,0:T(8,128)(2,1)S(1)}, bf16[2048,1792]{1,0:T(8,128)(2,1)}, bf16[2048,1792]{1,0:T(8,128)(2,1)}, bf16[1792,2048]{1,0:T(8,128)(2,1)}) %tuple.74), branch_computations={%region_4.4_spmd, %region_5.5_spmd} | conditional | flops 881315840 | bytes 23740424 | solution.py:55
  439.8 9.6 %all-to-all-done.1 = bf16[8,5,2048]{2,1,0:T(8,128)(2,1)S(1)} async-done(((bf16[8,5,2048]{2,1,0:T(8,128)(2,1)}), bf16[8,5,2048]{2,1,0:T(8,128)(2,1)S(1)}, u32[]{:S(2)}, u32[]{:S(2)}) %all-to-all-start.1) | async-done | bytes 163872 | tf_op jit(solution)/shard_map/while/body/eval_jaxpr/all_to_all | solution.py:56
  465.0 9.6 %all-to-all-done = bf16[8,5,2048]{2,1,0:T(8,128)(2,1)S(1)} async-done(((bf16[8,5,2048]{2,1,0:T(8,128)(2,1)}), bf16[8,5,2048]{2,1,0:T(8,128)(2,1)S(1)}, u32[]{:S(2)}, u32[]{:S(2)}) %all-to-all-start) | async-done | bytes 163872 | tf_op jit(solution)/shard_map/while/body/eval_jaxpr/all_to_all | solution.py:54
  474.5 13.1 %conditional.2 = (bf16[8,5,2048]{2,1,0:T(8,128)(2,1)}) conditional(s32[]{:T(128)} %convert_element_type.138, () %tuple.73, (bf16[8,5,2048]{2,1,0:T(8,128)(2,1)S(1)}, bf16[2048,1792]{1,0:T(8,128)(2,1)}, bf16[2048,1792]{1,0:T(8,128)(2,1)}, bf16[1792,2048]{1,0:T(8,128)(2,1)}) %tuple.74), branch_computations={%region_4.4_spmd, %region_5.5_spmd} | conditional | flops 881315840 | bytes 23740424 | solution.py:55
  491.1 9.6 %all-to-all-done.1 = bf16[8,5,2048]{2,1,0:T(8,128)(2,1)S(1)} async-done(((bf16[8,5,2048]{2,1,0:T(8,128)(2,1)}), bf16[8,5,2048]{2,1,0:T(8,128)(2,1)S(1)}, u32[]{:S(2)}, u32[]{:S(2)}) %all-to-all-start.1) | async-done | bytes 163872 | tf_op jit(solution)/shard_map/while/body/eval_jaxpr/all_to_all | solution.py:56
  516.2 9.6 %all-to-all-done = bf16[8,5,2048]{2,1,0:T(8,128)(2,1)S(1)} async-done(((bf16[8,5,2048]{2,1,0:T(8,128)(2,1)}), bf16[8,5,2048]{2,1,0:T(8,128)(2,1)S(1)}, u32[]{:S(2)}, u32[]{:S(2)}) %all-to-all-start) | async-done | bytes 163872 | tf_op jit(solution)/shard_map/while/body/eval_jaxpr/all_to_all | solution.py:54
  525.8 13.1 %conditional.2 = (bf16[8,5,2048]{2,1,0:T(8,128)(2,1)}) conditional(s32[]{:T(128)} %convert_element_type.138, () %tuple.73, (bf16[8,5,2048]{2,1,0:T(8,128)(2,1)S(1)}, bf16[2048,1792]{1,0:T(8,128)(2,1)}, bf16[2048,1792]{1,0:T(8,128)(2,1)}, bf16[1792,2048]{1,0:T(8,128)(2,1)}) %tuple.74), branch_computations={%region_4.4_spmd, %region_5.5_spmd} | conditional | flops 881315840 | bytes 23740424 | solution.py:55
  542.3 9.6 %all-to-all-done.1 = bf16[8,5,2048]{2,1,0:T(8,128)(2,1)S(1)} async-done(((bf16[8,5,2048]{2,1,0:T(8,128)(2,1)}), bf16[8,5,2048]{2,1,0:T(8,128)(2,1)S(1)}, u32[]{:S(2)}, u32[]{:S(2)}) %all-to-all-start.1) | async-done | bytes 163872 | tf_op jit(solution)/shard_map/while/body/eval_jaxpr/all_to_all | solution.py:56
  (337 shorter events, 311.6 us)
Async XLA Ops:
  5.5 14.6 %all-to-all-start = ((bf16[8,5,2048]{2,1,0:T(8,128)(2,1)}), bf16[8,5,2048]{2,1,0:T(8,128)(2,1)S(1)}, u32[]{:S(2)}, u32[]{:S(2)}) async-start(bf16[8,5,2048]{2,1,0:T(8,128)(2,1)} %bitcast.98), calls=%async_computation | async-start | bytes 524288 | tf_op jit(solution)/shard_map/while/body/eval_jaxpr/all_to_all | solution.py:54
  20.8 13.1 %all-to-all-start.1 = ((bf16[8,5,2048]{2,1,0:T(8,128)(2,1)}), bf16[8,5,2048]{2,1,0:T(8,128)(2,1)S(1)}, u32[]{:S(2)}, u32[]{:S(2)}) async-start(bf16[8,5,2048]{2,1,0:T(8,128)(2,1)} %get-tuple-element.654), calls=%async_computation.1 | async-start | bytes 524288 | tf_op jit(solution)/shard_map/while/body/eval_jaxpr/all_to_all | solution.py:56
  35.3 6.5 %collective-permute-start = (bf16[3,8,2048]{2,1,0:T(8,128)(2,1)S(1)}, bf16[3,8,2048]{2,1,0:T(8,128)(2,1)S(1)}, u32[]{:S(2)}, u32[]{:S(2)}) collective-permute-start(bf16[3,8,2048]{2,1,0:T(8,128)(2,1)S(1)} %maximum_select_fusion.2), channel_id=1, source_target_pairs={{0,8},{8,16},{16,24},{1,9},{9,17},{17,25},{2,10},{10,18},{18,26},{... | collective-permute-start | bytes 294920 | tf_op jit(solution)/shard_map/while/body/eval_jaxpr/ppermute | solution.py:16
  45.0 13.1 %all-to-all-start = ((bf16[8,5,2048]{2,1,0:T(8,128)(2,1)}), bf16[8,5,2048]{2,1,0:T(8,128)(2,1)S(1)}, u32[]{:S(2)}, u32[]{:S(2)}) async-start(bf16[8,5,2048]{2,1,0:T(8,128)(2,1)} %bitcast.98), calls=%async_computation | async-start | bytes 524288 | tf_op jit(solution)/shard_map/while/body/eval_jaxpr/all_to_all | solution.py:54
  58.8 13.1 %all-to-all-start.1 = ((bf16[8,5,2048]{2,1,0:T(8,128)(2,1)}), bf16[8,5,2048]{2,1,0:T(8,128)(2,1)S(1)}, u32[]{:S(2)}, u32[]{:S(2)}) async-start(bf16[8,5,2048]{2,1,0:T(8,128)(2,1)} %get-tuple-element.654), calls=%async_computation.1 | async-start | bytes 524288 | tf_op jit(solution)/shard_map/while/body/eval_jaxpr/all_to_all | solution.py:56
  83.0 13.1 %all-to-all-start = ((bf16[8,5,2048]{2,1,0:T(8,128)(2,1)}), bf16[8,5,2048]{2,1,0:T(8,128)(2,1)S(1)}, u32[]{:S(2)}, u32[]{:S(2)}) async-start(bf16[8,5,2048]{2,1,0:T(8,128)(2,1)} %bitcast.98), calls=%async_computation | async-start | bytes 524288 | tf_op jit(solution)/shard_map/while/body/eval_jaxpr/all_to_all | solution.py:54
  96.8 13.1 %all-to-all-start.1 = ((bf16[8,5,2048]{2,1,0:T(8,128)(2,1)}), bf16[8,5,2048]{2,1,0:T(8,128)(2,1)S(1)}, u32[]{:S(2)}, u32[]{:S(2)}) async-start(bf16[8,5,2048]{2,1,0:T(8,128)(2,1)} %get-tuple-element.654), calls=%async_computation.1 | async-start | bytes 524288 | tf_op jit(solution)/shard_map/while/body/eval_jaxpr/all_to_all | solution.py:56
  111.3 39.4 %collective-permute-start = (bf16[3,8,2048]{2,1,0:T(8,128)(2,1)S(1)}, bf16[3,8,2048]{2,1,0:T(8,128)(2,1)S(1)}, u32[]{:S(2)}, u32[]{:S(2)}) collective-permute-start(bf16[3,8,2048]{2,1,0:T(8,128)(2,1)S(1)} %maximum_select_fusion.2), channel_id=1, source_target_pairs={{0,8},{8,16},{16,24},{1,9},{9,17},{17,25},{2,10},{10,18},{18,26},{... | collective-permute-start | bytes 294920 | tf_op jit(solution)/shard_map/while/body/eval_jaxpr/ppermute | solution.py:16
  154.0 13.1 %all-to-all-start = ((bf16[8,5,2048]{2,1,0:T(8,128)(2,1)}), bf16[8,5,2048]{2,1,0:T(8,128)(2,1)S(1)}, u32[]{:S(2)}, u32[]{:S(2)}) async-start(bf16[8,5,2048]{2,1,0:T(8,128)(2,1)} %bitcast.98), calls=%async_computation | async-start | bytes 524288 | tf_op jit(solution)/shard_map/while/body/eval_jaxpr/all_to_all | solution.py:54
  180.1 13.1 %all-to-all-start.1 = ((bf16[8,5,2048]{2,1,0:T(8,128)(2,1)}), bf16[8,5,2048]{2,1,0:T(8,128)(2,1)S(1)}, u32[]{:S(2)}, u32[]{:S(2)}) async-start(bf16[8,5,2048]{2,1,0:T(8,128)(2,1)} %get-tuple-element.654), calls=%async_computation.1 | async-start | bytes 524288 | tf_op jit(solution)/shard_map/while/body/eval_jaxpr/all_to_all | solution.py:56
  194.5 7.4 %collective-permute-start = (bf16[3,8,2048]{2,1,0:T(8,128)(2,1)S(1)}, bf16[3,8,2048]{2,1,0:T(8,128)(2,1)S(1)}, u32[]{:S(2)}, u32[]{:S(2)}) collective-permute-start(bf16[3,8,2048]{2,1,0:T(8,128)(2,1)S(1)} %maximum_select_fusion.2), channel_id=1, source_target_pairs={{0,8},{8,16},{16,24},{1,9},{9,17},{17,25},{2,10},{10,18},{18,26},{... | collective-permute-start | bytes 294920 | tf_op jit(solution)/shard_map/while/body/eval_jaxpr/ppermute | solution.py:16
  205.2 13.1 %all-to-all-start = ((bf16[8,5,2048]{2,1,0:T(8,128)(2,1)}), bf16[8,5,2048]{2,1,0:T(8,128)(2,1)S(1)}, u32[]{:S(2)}, u32[]{:S(2)}) async-start(bf16[8,5,2048]{2,1,0:T(8,128)(2,1)} %bitcast.98), calls=%async_computation | async-start | bytes 524288 | tf_op jit(solution)/shard_map/while/body/eval_jaxpr/all_to_all | solution.py:54
  231.3 13.1 %all-to-all-start.1 = ((bf16[8,5,2048]{2,1,0:T(8,128)(2,1)}), bf16[8,5,2048]{2,1,0:T(8,128)(2,1)S(1)}, u32[]{:S(2)}, u32[]{:S(2)}) async-start(bf16[8,5,2048]{2,1,0:T(8,128)(2,1)} %get-tuple-element.654), calls=%async_computation.1 | async-start | bytes 524288 | tf_op jit(solution)/shard_map/while/body/eval_jaxpr/all_to_all | solution.py:56
  245.8 7.4 %collective-permute-start = (bf16[3,8,2048]{2,1,0:T(8,128)(2,1)S(1)}, bf16[3,8,2048]{2,1,0:T(8,128)(2,1)S(1)}, u32[]{:S(2)}, u32[]{:S(2)}) collective-permute-start(bf16[3,8,2048]{2,1,0:T(8,128)(2,1)S(1)} %maximum_select_fusion.2), channel_id=1, source_target_pairs={{0,8},{8,16},{16,24},{1,9},{9,17},{17,25},{2,10},{10,18},{18,26},{... | collective-permute-start | bytes 294920 | tf_op jit(solution)/shard_map/while/body/eval_jaxpr/ppermute | solution.py:16
  256.5 13.1 %all-to-all-start = ((bf16[8,5,2048]{2,1,0:T(8,128)(2,1)}), bf16[8,5,2048]{2,1,0:T(8,128)(2,1)S(1)}, u32[]{:S(2)}, u32[]{:S(2)}) async-start(bf16[8,5,2048]{2,1,0:T(8,128)(2,1)} %bitcast.98), calls=%async_computation | async-start | bytes 524288 | tf_op jit(solution)/shard_map/while/body/eval_jaxpr/all_to_all | solution.py:54
  282.6 13.1 %all-to-all-start.1 = ((bf16[8,5,2048]{2,1,0:T(8,128)(2,1)}), bf16[8,5,2048]{2,1,0:T(8,128)(2,1)S(1)}, u32[]{:S(2)}, u32[]{:S(2)}) async-start(bf16[8,5,2048]{2,1,0:T(8,128)(2,1)} %get-tuple-element.654), calls=%async_computation.1 | async-start | bytes 524288 | tf_op jit(solution)/shard_map/while/body/eval_jaxpr/all_to_all | solution.py:56
  297.0 7.4 %collective-permute-start = (bf16[3,8,2048]{2,1,0:T(8,128)(2,1)S(1)}, bf16[3,8,2048]{2,1,0:T(8,128)(2,1)S(1)}, u32[]{:S(2)}, u32[]{:S(2)}) collective-permute-start(bf16[3,8,2048]{2,1,0:T(8,128)(2,1)S(1)} %maximum_select_fusion.2), channel_id=1, source_target_pairs={{0,8},{8,16},{16,24},{1,9},{9,17},{17,25},{2,10},{10,18},{18,26},{... | collective-permute-start | bytes 294920 | tf_op jit(solution)/shard_map/while/body/eval_jaxpr/ppermute | solution.py:16
  307.7 13.1 %all-to-all-start = ((bf16[8,5,2048]{2,1,0:T(8,128)(2,1)}), bf16[8,5,2048]{2,1,0:T(8,128)(2,1)S(1)}, u32[]{:S(2)}, u32[]{:S(2)}) async-start(bf16[8,5,2048]{2,1,0:T(8,128)(2,1)} %bitcast.98), calls=%async_computation | async-start | bytes 524288 | tf_op jit(solution)/shard_map/while/body/eval_jaxpr/all_to_all | solution.py:54
  333.9 13.1 %all-to-all-start.1 = ((bf16[8,5,2048]{2,1,0:T(8,128)(2,1)}), bf16[8,5,2048]{2,1,0:T(8,128)(2,1)S(1)}, u32[]{:S(2)}, u32[]{:S(2)}) async-start(bf16[8,5,2048]{2,1,0:T(8,128)(2,1)} %get-tuple-element.654), calls=%async_computation.1 | async-start | bytes 524288 | tf_op jit(solution)/shard_map/while/body/eval_jaxpr/all_to_all | solution.py:56
  348.3 7.4 %collective-permute-start = (bf16[3,8,2048]{2,1,0:T(8,128)(2,1)S(1)}, bf16[3,8,2048]{2,1,0:T(8,128)(2,1)S(1)}, u32[]{:S(2)}, u32[]{:S(2)}) collective-permute-start(bf16[3,8,2048]{2,1,0:T(8,128)(2,1)S(1)} %maximum_select_fusion.2), channel_id=1, source_target_pairs={{0,8},{8,16},{16,24},{1,9},{9,17},{17,25},{2,10},{10,18},{18,26},{... | collective-permute-start | bytes 294920 | tf_op jit(solution)/shard_map/while/body/eval_jaxpr/ppermute | solution.py:16
  359.0 13.1 %all-to-all-start = ((bf16[8,5,2048]{2,1,0:T(8,128)(2,1)}), bf16[8,5,2048]{2,1,0:T(8,128)(2,1)S(1)}, u32[]{:S(2)}, u32[]{:S(2)}) async-start(bf16[8,5,2048]{2,1,0:T(8,128)(2,1)} %bitcast.98), calls=%async_computation | async-start | bytes 524288 | tf_op jit(solution)/shard_map/while/body/eval_jaxpr/all_to_all | solution.py:54
  385.1 13.1 %all-to-all-start.1 = ((bf16[8,5,2048]{2,1,0:T(8,128)(2,1)}), bf16[8,5,2048]{2,1,0:T(8,128)(2,1)S(1)}, u32[]{:S(2)}, u32[]{:S(2)}) async-start(bf16[8,5,2048]{2,1,0:T(8,128)(2,1)} %get-tuple-element.654), calls=%async_computation.1 | async-start | bytes 524288 | tf_op jit(solution)/shard_map/while/body/eval_jaxpr/all_to_all | solution.py:56
  399.6 7.4 %collective-permute-start = (bf16[3,8,2048]{2,1,0:T(8,128)(2,1)S(1)}, bf16[3,8,2048]{2,1,0:T(8,128)(2,1)S(1)}, u32[]{:S(2)}, u32[]{:S(2)}) collective-permute-start(bf16[3,8,2048]{2,1,0:T(8,128)(2,1)S(1)} %maximum_select_fusion.2), channel_id=1, source_target_pairs={{0,8},{8,16},{16,24},{1,9},{9,17},{17,25},{2,10},{10,18},{18,26},{... | collective-permute-start | bytes 294920 | tf_op jit(solution)/shard_map/while/body/eval_jaxpr/ppermute | solution.py:16
  410.2 13.1 %all-to-all-start = ((bf16[8,5,2048]{2,1,0:T(8,128)(2,1)}), bf16[8,5,2048]{2,1,0:T(8,128)(2,1)S(1)}, u32[]{:S(2)}, u32[]{:S(2)}) async-start(bf16[8,5,2048]{2,1,0:T(8,128)(2,1)} %bitcast.98), calls=%async_computation | async-start | bytes 524288 | tf_op jit(solution)/shard_map/while/body/eval_jaxpr/all_to_all | solution.py:54
  436.4 13.1 %all-to-all-start.1 = ((bf16[8,5,2048]{2,1,0:T(8,128)(2,1)}), bf16[8,5,2048]{2,1,0:T(8,128)(2,1)S(1)}, u32[]{:S(2)}, u32[]{:S(2)}) async-start(bf16[8,5,2048]{2,1,0:T(8,128)(2,1)} %get-tuple-element.654), calls=%async_computation.1 | async-start | bytes 524288 | tf_op jit(solution)/shard_map/while/body/eval_jaxpr/all_to_all | solution.py:56
  450.8 7.4 %collective-permute-start = (bf16[3,8,2048]{2,1,0:T(8,128)(2,1)S(1)}, bf16[3,8,2048]{2,1,0:T(8,128)(2,1)S(1)}, u32[]{:S(2)}, u32[]{:S(2)}) collective-permute-start(bf16[3,8,2048]{2,1,0:T(8,128)(2,1)S(1)} %maximum_select_fusion.2), channel_id=1, source_target_pairs={{0,8},{8,16},{16,24},{1,9},{9,17},{17,25},{2,10},{10,18},{18,26},{... | collective-permute-start | bytes 294920 | tf_op jit(solution)/shard_map/while/body/eval_jaxpr/ppermute | solution.py:16
  461.5 13.1 %all-to-all-start = ((bf16[8,5,2048]{2,1,0:T(8,128)(2,1)}), bf16[8,5,2048]{2,1,0:T(8,128)(2,1)S(1)}, u32[]{:S(2)}, u32[]{:S(2)}) async-start(bf16[8,5,2048]{2,1,0:T(8,128)(2,1)} %bitcast.98), calls=%async_computation | async-start | bytes 524288 | tf_op jit(solution)/shard_map/while/body/eval_jaxpr/all_to_all | solution.py:54
  487.6 13.1 %all-to-all-start.1 = ((bf16[8,5,2048]{2,1,0:T(8,128)(2,1)}), bf16[8,5,2048]{2,1,0:T(8,128)(2,1)S(1)}, u32[]{:S(2)}, u32[]{:S(2)}) async-start(bf16[8,5,2048]{2,1,0:T(8,128)(2,1)} %get-tuple-element.654), calls=%async_computation.1 | async-start | bytes 524288 | tf_op jit(solution)/shard_map/while/body/eval_jaxpr/all_to_all | solution.py:56
  502.1 7.4 %collective-permute-start = (bf16[3,8,2048]{2,1,0:T(8,128)(2,1)S(1)}, bf16[3,8,2048]{2,1,0:T(8,128)(2,1)S(1)}, u32[]{:S(2)}, u32[]{:S(2)}) collective-permute-start(bf16[3,8,2048]{2,1,0:T(8,128)(2,1)S(1)} %maximum_select_fusion.2), channel_id=1, source_target_pairs={{0,8},{8,16},{16,24},{1,9},{9,17},{17,25},{2,10},{10,18},{18,26},{... | collective-permute-start | bytes 294920 | tf_op jit(solution)/shard_map/while/body/eval_jaxpr/ppermute | solution.py:16
  512.7 13.1 %all-to-all-start = ((bf16[8,5,2048]{2,1,0:T(8,128)(2,1)}), bf16[8,5,2048]{2,1,0:T(8,128)(2,1)S(1)}, u32[]{:S(2)}, u32[]{:S(2)}) async-start(bf16[8,5,2048]{2,1,0:T(8,128)(2,1)} %bitcast.98), calls=%async_computation | async-start | bytes 524288 | tf_op jit(solution)/shard_map/while/body/eval_jaxpr/all_to_all | solution.py:54
  538.9 13.1 %all-to-all-start.1 = ((bf16[8,5,2048]{2,1,0:T(8,128)(2,1)}), bf16[8,5,2048]{2,1,0:T(8,128)(2,1)S(1)}, u32[]{:S(2)}, u32[]{:S(2)}) async-start(bf16[8,5,2048]{2,1,0:T(8,128)(2,1)} %get-tuple-element.654), calls=%async_computation.1 | async-start | bytes 524288 | tf_op jit(solution)/shard_map/while/body/eval_jaxpr/all_to_all | solution.py:56
  553.3 6.5 %collective-permute-start = (bf16[3,8,2048]{2,1,0:T(8,128)(2,1)S(1)}, bf16[3,8,2048]{2,1,0:T(8,128)(2,1)S(1)}, u32[]{:S(2)}, u32[]{:S(2)}) collective-permute-start(bf16[3,8,2048]{2,1,0:T(8,128)(2,1)S(1)} %maximum_select_fusion.2), channel_id=1, source_target_pairs={{0,8},{8,16},{16,24},{1,9},{9,17},{17,25},{2,10},{10,18},{18,26},{... | collective-permute-start | bytes 294920 | tf_op jit(solution)/shard_map/while/body/eval_jaxpr/ppermute | solution.py:16
  (3 other events, 9.4 us)
where the time goes:
time: 564 us; the launch traced here: 561 us
  waiting for transfers between devices  307 us (54%)
  matrix products  97.6 us (17%)
  starting transfers between devices  90.8 us (16%)
  local copies, waits for them, and re-layouts  33.4 us (6%)
  other arithmetic  29.3 us (5%)
    all_to_all x11, waiting for transfers between devices, run_experts(): lax.all_to_all(computed, 'expert', split_axis=0, concat_axis=0, tiled=True)  106 us
    all_to_all x11, waiting for transfers between devices, run_experts(): lax.all_to_all(outgoing, 'expert', split_axis=0, concat_axis=0, tiled=True)  105 us
    ppermute x11, waiting for transfers between devices, shifted(): return lax.ppermute(value, axis, pairs)  96.5 us
    dot_general x8, matrix products, expert_rows(): jnp.dot(hidden, down_mat, preferred_element_type=jnp.float32)  62.1 us
    all_to_all x11, starting transfers between devices, run_experts(): lax.all_to_all(outgoing, 'expert', split_axis=0, concat_axis=0, tiled=True)  39 us
    all_to_all x11, starting transfers between devices, run_experts(): lax.all_to_all(computed, 'expert', split_axis=0, concat_axis=0, tiled=True)  37.5 us
    dot_general x8, matrix products, expert_rows(): gate_vals = jnp.dot(flat_rows, gate_mat, preferred_element_type=jnp.float32)  35.5 us
    ppermute x11, starting transfers between devices, shifted(): return lax.ppermute(value, axis, pairs)  14.2 us
  transfers between devices with their start and end apart: 33, of which 33 were waited for; matrix products, arithmetic and copies ran while one was open for 0% of the time, Pallas kernels for 0%

commit v1 on v0

--- a/solution.py
+++ b/solution.py
@@ -51,7 +51,20 @@
         return jnp.zeros(received.shape, jnp.bfloat16)
 
     def run_experts(outgoing, active):
-        received = lax.all_to_all(outgoing, "expert", split_axis=0, concat_axis=0, tiled=True)
+        ways, here = (lax.axis_size("expert"), lax.axis_index("expert"))
+        width = outgoing.shape[0] // ways
+        shape = list(outgoing.shape)
+        shape[0] = width
+        height = shape[0]
+        shape[0] = height * ways
+        received = jnp.zeros(shape, outgoing.dtype)
+        for mask in range(ways):
+            part = lax.dynamic_slice_in_dim(outgoing, (here ^ mask) * width, width, axis=0)
+            if mask:
+                part = lax.ppermute(part, "expert", [(d, d ^ mask) for d in range(ways)])
+            received = lax.dynamic_update_slice_in_dim(
+                received, part, (here ^ mask) * height, axis=0
+            )
         computed = lax.cond(active, expert_rows, skip_rows, received)
         returned = lax.all_to_all(computed, "expert", split_axis=0, concat_axis=0, tiled=True)
         return returned

time: 564 us -> 542 us (0.961)
  waiting for transfers between devices: 307 us -> 240 us
  starting transfers between devices: 90.8 us -> 142 us
  local copies, waits for them, and re-layouts: 33.4 us -> 26.8 us
    all_to_all x11 -> x0, waiting for transfers between devices: 105 us -> none  [run_experts(): lax.all_to_all(outgoing, 'expert', split_axis=0, concat_axis=0, tiled=True)]
    ppermute x0 -> x77, starting transfers between devices: none -> 90 us  [run_experts(): part = lax.ppermute(part, 'expert', [(d, d ^ mask) for d in range(ways)])]
    all_to_all x11 -> x0, starting transfers between devices: 39 us -> none  [run_experts(): lax.all_to_all(outgoing, 'expert', split_axis=0, concat_axis=0, tiled=True)]
    ppermute x0 -> x77, waiting for transfers between devices: none -> 37.1 us  [run_experts(): part = lax.ppermute(part, 'expert', [(d, d ^ mask) for d in range(ways)])]
    broadcast_in_dim x11, local copies, waits for them, and re-layouts: 7.93 us -> 0.21 us  [advance(): outgoing = jnp.repeat(buffer, shards, axis=0)]
  transfers between devices with their start and end apart: 33 -> 99, of which waited for: 33 -> 45; matrix products, arithmetic and copies ran while one was open for 0% -> 0% of each run, Pallas kernels for 0% -> 0%
where the time goes in v1:
time: 542 us; the launch traced here: 539 us
  waiting for transfers between devices  240 us (44%)
  starting transfers between devices  142 us (26%)
  matrix products  97.6 us (18%)
  other arithmetic  29.2 us (5%)
  local copies, waits for them, and re-layouts  26.8 us (5%)
    all_to_all x11, waiting for transfers between devices, run_experts(): lax.all_to_all(computed, 'expert', split_axis=0, concat_axis=0, tiled=True)  106 us
    ppermute x11, waiting for transfers between devices, shifted(): return lax.ppermute(value, axis, pairs)  97 us
    ppermute x77, starting transfers between devices, run_experts(): part = lax.ppermute(part, 'expert', [(d, d ^ mask) for d in range(ways)])  90 us
    dot_general x8, matrix products, expert_rows(): jnp.dot(hidden, down_mat, preferred_element_type=jnp.float32)  62.1 us
    all_to_all x11, starting transfers between devices, run_experts(): lax.all_to_all(computed, 'expert', split_axis=0, concat_axis=0, tiled=True)  38.1 us
    ppermute x77, waiting for transfers between devices, run_experts(): part = lax.ppermute(part, 'expert', [(d, d ^ mask) for d in range(ways)])  37.1 us
    dot_general x8, matrix products, expert_rows(): gate_vals = jnp.dot(flat_rows, gate_mat, preferred_element_type=jnp.float32)  35.5 us
    ppermute x11, starting transfers between devices, shifted(): return lax.ppermute(value, axis, pairs)  14.2 us
  transfers between devices with their start and end apart: 99, of which 45 were waited for; matrix products, arithmetic and copies ran while one was open for 0% of the time, Pallas kernels for 0%

profile of v1, /device:TPU:6, one launch (start us, length us, event | category | flops | bytes accessed | tf_op | source)
XLA Modules:
  0.0 539.5 jit_solution(4210887245931107998)
XLA Ops:
  2.2 536.6 %while.17 = (s32[]{:T(128)}, bf16[3,8,2048]{2,1,0:T(8,128)(2,1)S(1)}, bf16[8,8,2048]{2,1,0:T(8,128)(2,1)S(1)}, pred[]{:T(512)}, pred[]{:T(512)}, /*index=5*/s32[...) while((s32[]{:T(128)}, ...), condition=%wide.region_7.8_spmd, body=%wide.region_0.7_spmd.sunk | while | flops 881903936 | bytes 27907788 | solution.py:122
  22.5 9.6 %all-to-all-done = bf16[8,5,2048]{2,1,0:T(8,128)(2,1)S(1)} async-done(((bf16[8,5,2048]{2,1,0:T(8,128)(2,1)}), bf16[8,5,2048]{2,1,0:T(8,128)(2,1)S(1)}, u32[]{:S(2)}, u32[]{:S(2)}) %all-to-all-start) | async-done | bytes 163872 | tf_op jit(solution)/shard_map/while/body/eval_jaxpr/all_to_all | solution.py:69
  58.3 9.7 %all-to-all-done = bf16[8,5,2048]{2,1,0:T(8,128)(2,1)S(1)} async-done(((bf16[8,5,2048]{2,1,0:T(8,128)(2,1)}), bf16[8,5,2048]{2,1,0:T(8,128)(2,1)S(1)}, u32[]{:S(2)}, u32[]{:S(2)}) %all-to-all-start) | async-done | bytes 163872 | tf_op jit(solution)/shard_map/while/body/eval_jaxpr/all_to_all | solution.py:69
  94.2 9.7 %all-to-all-done = bf16[8,5,2048]{2,1,0:T(8,128)(2,1)S(1)} async-done(((bf16[8,5,2048]{2,1,0:T(8,128)(2,1)}), bf16[8,5,2048]{2,1,0:T(8,128)(2,1)S(1)}, u32[]{:S(2)}, u32[]{:S(2)}) %all-to-all-start) | async-done | bytes 163872 | tf_op jit(solution)/shard_map/while/body/eval_jaxpr/all_to_all | solution.py:69
  106.6 38.6 %collective-permute-done.7 = bf16[3,8,2048]{2,1,0:T(8,128)(2,1)S(1)} collective-permute-done((bf16[3,8,2048]{2,1,0:T(8,128)(2,1)S(1)}, bf16[3,8,2048]{2,1,0:T(8,128)(2,1)S(1)}, u32[]{:S(2)}, u32[]{:S(2)}) %collective-permute-start.7) | collective-permute-done | bytes 98336 | tf_op jit(solution)/shard_map/while/body/eval_jaxpr/ppermute | solution.py:16
  159.4 13.3 %conditional.2 = (bf16[8,5,2048]{2,1,0:T(8,128)(2,1)}) conditional(s32[]{:T(128)} %convert_element_type.142, () %tuple.86, (s32[]{:T(128)}, bf16[8,5,2048]{2,1,0:T(8,128)(2,1)S(1)}, bf16[1,5,2048]{2,1,0:T(8,128)(2,1)S(1)}, s32[]{:T(128)}, bf16[1,5,2048]{2,1,0:T(8,128)(2,1)S(1)}, /*index=5*/s32[]{:T(128)}, bf16[1,5,2048]{2,1,0:T(8,128)(2,1)S(1)}, ...), branch_computations={%region_4.4_spmd, %region_5.5_spmd} | conditional | flops 881315840 | bytes 24428620 | solution.py:68
  164.1 7.8 %convolution_convert_fusion = bf16[40,2048]{1,0:T(8,128)(2,1)S(1)} fusion(bf16[1792,2048]{1,0:T(8,128)(2,1)} %get-tuple-element.515, bf16[40,2048]{1,0:T(8,128)(2,1)S(1)} %reshape.154, bf16[2048,1792]{1,0:T(8,128)(2,1)} %get-tuple-element.514, f32[40,1792]{1,0:T(8,128)S(1)} %fusion.25), kind=kOutput, calls=%fused_computation.6 | convolution fusion | flops 587714560 | bytes 15294464 | tf_op jit(solution)/shard_map/while/body/eval_jaxpr/cond/branch_1_fun/dot_general | solution.py:45
  176.1 9.6 %all-to-all-done = bf16[8,5,2048]{2,1,0:T(8,128)(2,1)S(1)} async-done(((bf16[8,5,2048]{2,1,0:T(8,128)(2,1)}), bf16[8,5,2048]{2,1,0:T(8,128)(2,1)S(1)}, u32[]{:S(2)}, u32[]{:S(2)}) %all-to-all-start) | async-done | bytes 163872 | tf_op jit(solution)/shard_map/while/body/eval_jaxpr/all_to_all | solution.py:69
  188.4 6.1 %collective-permute-done.7 = bf16[3,8,2048]{2,1,0:T(8,128)(2,1)S(1)} collective-permute-done((bf16[3,8,2048]{2,1,0:T(8,128)(2,1)S(1)}, bf16[3,8,2048]{2,1,0:T(8,128)(2,1)S(1)}, u32[]{:S(2)}, u32[]{:S(2)}) %collective-permute-start.7) | collective-permute-done | bytes 98336 | tf_op jit(solution)/shard_map/while/body/eval_jaxpr/ppermute | solution.py:16
  208.7 13.3 %conditional.2 = (bf16[8,5,2048]{2,1,0:T(8,128)(2,1)}) conditional(s32[]{:T(128)} %convert_element_type.142, () %tuple.86, (s32[]{:T(128)}, bf16[8,5,2048]{2,1,0:T(8,128)(2,1)S(1)}, bf16[1,5,2048]{2,1,0:T(8,128)(2,1)S(1)}, s32[]{:T(128)}, bf16[1,5,2048]{2,1,0:T(8,128)(2,1)S(1)}, /*index=5*/s32[]{:T(128)}, bf16[1,5,2048]{2,1,0:T(8,128)(2,1)S(1)}, ...), branch_computations={%region_4.4_spmd, %region_5.5_spmd} | conditional | flops 881315840 | bytes 24428620 | solution.py:68
  213.4 7.8 %convolution_convert_fusion = bf16[40,2048]{1,0:T(8,128)(2,1)S(1)} fusion(bf16[1792,2048]{1,0:T(8,128)(2,1)} %get-tuple-element.515, bf16[40,2048]{1,0:T(8,128)(2,1)S(1)} %reshape.154, bf16[2048,1792]{1,0:T(8,128)(2,1)} %get-tuple-element.514, f32[40,1792]{1,0:T(8,128)S(1)} %fusion.25), kind=kOutput, calls=%fused_computation.6 | convolution fusion | flops 587714560 | bytes 15294464 | tf_op jit(solution)/shard_map/while/body/eval_jaxpr/cond/branch_1_fun/dot_general | solution.py:45
  225.4 9.6 %all-to-all-done = bf16[8,5,2048]{2,1,0:T(8,128)(2,1)S(1)} async-done(((bf16[8,5,2048]{2,1,0:T(8,128)(2,1)}), bf16[8,5,2048]{2,1,0:T(8,128)(2,1)S(1)}, u32[]{:S(2)}, u32[]{:S(2)}) %all-to-all-start) | async-done | bytes 163872 | tf_op jit(solution)/shard_map/while/body/eval_jaxpr/all_to_all | solution.py:69
  258.0 13.3 %conditional.2 = (bf16[8,5,2048]{2,1,0:T(8,128)(2,1)}) conditional(s32[]{:T(128)} %convert_element_type.142, () %tuple.86, (s32[]{:T(128)}, bf16[8,5,2048]{2,1,0:T(8,128)(2,1)S(1)}, bf16[1,5,2048]{2,1,0:T(8,128)(2,1)S(1)}, s32[]{:T(128)}, bf16[1,5,2048]{2,1,0:T(8,128)(2,1)S(1)}, /*index=5*/s32[]{:T(128)}, bf16[1,5,2048]{2,1,0:T(8,128)(2,1)S(1)}, ...), branch_computations={%region_4.4_spmd, %region_5.5_spmd} | conditional | flops 881315840 | bytes 24428620 | solution.py:68
  262.7 7.8 %convolution_convert_fusion = bf16[40,2048]{1,0:T(8,128)(2,1)S(1)} fusion(bf16[1792,2048]{1,0:T(8,128)(2,1)} %get-tuple-element.515, bf16[40,2048]{1,0:T(8,128)(2,1)S(1)} %reshape.154, bf16[2048,1792]{1,0:T(8,128)(2,1)} %get-tuple-element.514, f32[40,1792]{1,0:T(8,128)S(1)} %fusion.25), kind=kOutput, calls=%fused_computation.6 | convolution fusion | flops 587714560 | bytes 15294464 | tf_op jit(solution)/shard_map/while/body/eval_jaxpr/cond/branch_1_fun/dot_general | solution.py:45
  274.7 9.6 %all-to-all-done = bf16[8,5,2048]{2,1,0:T(8,128)(2,1)S(1)} async-done(((bf16[8,5,2048]{2,1,0:T(8,128)(2,1)}), bf16[8,5,2048]{2,1,0:T(8,128)(2,1)S(1)}, u32[]{:S(2)}, u32[]{:S(2)}) %all-to-all-start) | async-done | bytes 163872 | tf_op jit(solution)/shard_map/while/body/eval_jaxpr/all_to_all | solution.py:69
  287.0 6.1 %collective-permute-done.7 = bf16[3,8,2048]{2,1,0:T(8,128)(2,1)S(1)} collective-permute-done((bf16[3,8,2048]{2,1,0:T(8,128)(2,1)S(1)}, bf16[3,8,2048]{2,1,0:T(8,128)(2,1)S(1)}, u32[]{:S(2)}, u32[]{:S(2)}) %collective-permute-start.7) | collective-permute-done | bytes 98336 | tf_op jit(solution)/shard_map/while/body/eval_jaxpr/ppermute | solution.py:16
  307.3 13.3 %conditional.2 = (bf16[8,5,2048]{2,1,0:T(8,128)(2,1)}) conditional(s32[]{:T(128)} %convert_element_type.142, () %tuple.86, (s32[]{:T(128)}, bf16[8,5,2048]{2,1,0:T(8,128)(2,1)S(1)}, bf16[1,5,2048]{2,1,0:T(8,128)(2,1)S(1)}, s32[]{:T(128)}, bf16[1,5,2048]{2,1,0:T(8,128)(2,1)S(1)}, /*index=5*/s32[]{:T(128)}, bf16[1,5,2048]{2,1,0:T(8,128)(2,1)S(1)}, ...), branch_computations={%region_4.4_spmd, %region_5.5_spmd} | conditional | flops 881315840 | bytes 24428620 | solution.py:68
  312.0 7.8 %convolution_convert_fusion = bf16[40,2048]{1,0:T(8,128)(2,1)S(1)} fusion(bf16[1792,2048]{1,0:T(8,128)(2,1)} %get-tuple-element.515, bf16[40,2048]{1,0:T(8,128)(2,1)S(1)} %reshape.154, bf16[2048,1792]{1,0:T(8,128)(2,1)} %get-tuple-element.514, f32[40,1792]{1,0:T(8,128)S(1)} %fusion.25), kind=kOutput, calls=%fused_computation.6 | convolution fusion | flops 587714560 | bytes 15294464 | tf_op jit(solution)/shard_map/while/body/eval_jaxpr/cond/branch_1_fun/dot_general | solution.py:45
  324.0 9.6 %all-to-all-done = bf16[8,5,2048]{2,1,0:T(8,128)(2,1)S(1)} async-done(((bf16[8,5,2048]{2,1,0:T(8,128)(2,1)}), bf16[8,5,2048]{2,1,0:T(8,128)(2,1)S(1)}, u32[]{:S(2)}, u32[]{:S(2)}) %all-to-all-start) | async-done | bytes 163872 | tf_op jit(solution)/shard_map/while/body/eval_jaxpr/all_to_all | solution.py:69
  356.6 13.3 %conditional.2 = (bf16[8,5,2048]{2,1,0:T(8,128)(2,1)}) conditional(s32[]{:T(128)} %convert_element_type.142, () %tuple.86, (s32[]{:T(128)}, bf16[8,5,2048]{2,1,0:T(8,128)(2,1)S(1)}, bf16[1,5,2048]{2,1,0:T(8,128)(2,1)S(1)}, s32[]{:T(128)}, bf16[1,5,2048]{2,1,0:T(8,128)(2,1)S(1)}, /*index=5*/s32[]{:T(128)}, bf16[1,5,2048]{2,1,0:T(8,128)(2,1)S(1)}, ...), branch_computations={%region_4.4_spmd, %region_5.5_spmd} | conditional | flops 881315840 | bytes 24428620 | solution.py:68
  361.3 7.8 %convolution_convert_fusion = bf16[40,2048]{1,0:T(8,128)(2,1)S(1)} fusion(bf16[1792,2048]{1,0:T(8,128)(2,1)} %get-tuple-element.515, bf16[40,2048]{1,0:T(8,128)(2,1)S(1)} %reshape.154, bf16[2048,1792]{1,0:T(8,128)(2,1)} %get-tuple-element.514, f32[40,1792]{1,0:T(8,128)S(1)} %fusion.25), kind=kOutput, calls=%fused_computation.6 | convolution fusion | flops 587714560 | bytes 15294464 | tf_op jit(solution)/shard_map/while/body/eval_jaxpr/cond/branch_1_fun/dot_general | solution.py:45
  373.3 9.6 %all-to-all-done = bf16[8,5,2048]{2,1,0:T(8,128)(2,1)S(1)} async-done(((bf16[8,5,2048]{2,1,0:T(8,128)(2,1)}), bf16[8,5,2048]{2,1,0:T(8,128)(2,1)S(1)}, u32[]{:S(2)}, u32[]{:S(2)}) %all-to-all-start) | async-done | bytes 163872 | tf_op jit(solution)/shard_map/while/body/eval_jaxpr/all_to_all | solution.py:69
  405.9 13.3 %conditional.2 = (bf16[8,5,2048]{2,1,0:T(8,128)(2,1)}) conditional(s32[]{:T(128)} %convert_element_type.142, () %tuple.86, (s32[]{:T(128)}, bf16[8,5,2048]{2,1,0:T(8,128)(2,1)S(1)}, bf16[1,5,2048]{2,1,0:T(8,128)(2,1)S(1)}, s32[]{:T(128)}, bf16[1,5,2048]{2,1,0:T(8,128)(2,1)S(1)}, /*index=5*/s32[]{:T(128)}, bf16[1,5,2048]{2,1,0:T(8,128)(2,1)S(1)}, ...), branch_computations={%region_4.4_spmd, %region_5.5_spmd} | conditional | flops 881315840 | bytes 24428620 | solution.py:68
  410.6 7.8 %convolution_convert_fusion = bf16[40,2048]{1,0:T(8,128)(2,1)S(1)} fusion(bf16[1792,2048]{1,0:T(8,128)(2,1)} %get-tuple-element.515, bf16[40,2048]{1,0:T(8,128)(2,1)S(1)} %reshape.154, bf16[2048,1792]{1,0:T(8,128)(2,1)} %get-tuple-element.514, f32[40,1792]{1,0:T(8,128)S(1)} %fusion.25), kind=kOutput, calls=%fused_computation.6 | convolution fusion | flops 587714560 | bytes 15294464 | tf_op jit(solution)/shard_map/while/body/eval_jaxpr/cond/branch_1_fun/dot_general | solution.py:45
  422.6 9.6 %all-to-all-done = bf16[8,5,2048]{2,1,0:T(8,128)(2,1)S(1)} async-done(((bf16[8,5,2048]{2,1,0:T(8,128)(2,1)}), bf16[8,5,2048]{2,1,0:T(8,128)(2,1)S(1)}, u32[]{:S(2)}, u32[]{:S(2)}) %all-to-all-start) | async-done | bytes 163872 | tf_op jit(solution)/shard_map/while/body/eval_jaxpr/all_to_all | solution.py:69
  455.2 13.3 %conditional.2 = (bf16[8,5,2048]{2,1,0:T(8,128)(2,1)}) conditional(s32[]{:T(128)} %convert_element_type.142, () %tuple.86, (s32[]{:T(128)}, bf16[8,5,2048]{2,1,0:T(8,128)(2,1)S(1)}, bf16[1,5,2048]{2,1,0:T(8,128)(2,1)S(1)}, s32[]{:T(128)}, bf16[1,5,2048]{2,1,0:T(8,128)(2,1)S(1)}, /*index=5*/s32[]{:T(128)}, bf16[1,5,2048]{2,1,0:T(8,128)(2,1)S(1)}, ...), branch_computations={%region_4.4_spmd, %region_5.5_spmd} | conditional | flops 881315840 | bytes 24428620 | solution.py:68
  459.9 7.8 %convolution_convert_fusion = bf16[40,2048]{1,0:T(8,128)(2,1)S(1)} fusion(bf16[1792,2048]{1,0:T(8,128)(2,1)} %get-tuple-element.515, bf16[40,2048]{1,0:T(8,128)(2,1)S(1)} %reshape.154, bf16[2048,1792]{1,0:T(8,128)(2,1)} %get-tuple-element.514, f32[40,1792]{1,0:T(8,128)S(1)} %fusion.25), kind=kOutput, calls=%fused_computation.6 | convolution fusion | flops 587714560 | bytes 15294464 | tf_op jit(solution)/shard_map/while/body/eval_jaxpr/cond/branch_1_fun/dot_general | solution.py:45
  471.9 9.6 %all-to-all-done = bf16[8,5,2048]{2,1,0:T(8,128)(2,1)S(1)} async-done(((bf16[8,5,2048]{2,1,0:T(8,128)(2,1)}), bf16[8,5,2048]{2,1,0:T(8,128)(2,1)S(1)}, u32[]{:S(2)}, u32[]{:S(2)}) %all-to-all-start) | async-done | bytes 163872 | tf_op jit(solution)/shard_map/while/body/eval_jaxpr/all_to_all | solution.py:69
  484.3 6.1 %collective-permute-done.7 = bf16[3,8,2048]{2,1,0:T(8,128)(2,1)S(1)} collective-permute-done((bf16[3,8,2048]{2,1,0:T(8,128)(2,1)S(1)}, bf16[3,8,2048]{2,1,0:T(8,128)(2,1)S(1)}, u32[]{:S(2)}, u32[]{:S(2)}) %collective-permute-start.7) | collective-permute-done | bytes 98336 | tf_op jit(solution)/shard_map/while/body/eval_jaxpr/ppermute | solution.py:16
  504.5 13.3 %conditional.2 = (bf16[8,5,2048]{2,1,0:T(8,128)(2,1)}) conditional(s32[]{:T(128)} %convert_element_type.142, () %tuple.86, (s32[]{:T(128)}, bf16[8,5,2048]{2,1,0:T(8,128)(2,1)S(1)}, bf16[1,5,2048]{2,1,0:T(8,128)(2,1)S(1)}, s32[]{:T(128)}, bf16[1,5,2048]{2,1,0:T(8,128)(2,1)S(1)}, /*index=5*/s32[]{:T(128)}, bf16[1,5,2048]{2,1,0:T(8,128)(2,1)S(1)}, ...), branch_computations={%region_4.4_spmd, %region_5.5_spmd} | conditional | flops 881315840 | bytes 24428620 | solution.py:68
  509.2 7.8 %convolution_convert_fusion = bf16[40,2048]{1,0:T(8,128)(2,1)S(1)} fusion(bf16[1792,2048]{1,0:T(8,128)(2,1)} %get-tuple-element.515, bf16[40,2048]{1,0:T(8,128)(2,1)S(1)} %reshape.154, bf16[2048,1792]{1,0:T(8,128)(2,1)} %get-tuple-element.514, f32[40,1792]{1,0:T(8,128)S(1)} %fusion.25), kind=kOutput, calls=%fused_computation.6 | convolution fusion | flops 587714560 | bytes 15294464 | tf_op jit(solution)/shard_map/while/body/eval_jaxpr/cond/branch_1_fun/dot_general | solution.py:45
  521.2 9.6 %all-to-all-done = bf16[8,5,2048]{2,1,0:T(8,128)(2,1)S(1)} async-done(((bf16[8,5,2048]{2,1,0:T(8,128)(2,1)}), bf16[8,5,2048]{2,1,0:T(8,128)(2,1)S(1)}, u32[]{:S(2)}, u32[]{:S(2)}) %all-to-all-start) | async-done | bytes 163872 | tf_op jit(solution)/shard_map/while/body/eval_jaxpr/all_to_all | solution.py:69
  (552 shorter events, 313.2 us)
Async XLA Ops:
  5.0 8.2 %collective-permute-start.1 = (bf16[1,5,2048]{2,1,0:T(8,128)(2,1)S(1)}, bf16[1,5,2048]{2,1,0:T(8,128)(2,1)S(1)}, u32[]{:S(2)}, u32[]{:S(2)}) collective-permute-start(bf16[1,5,2048]{2,1,0:T(8,128)(2,1)S(1)} %get-tuple-element.760), channel_id=1, source_target_pairs={{0,2},{1,3},{2,0},{3,1},{4,6},{5,7},{6,4},{7,5},{8,10},{9,11},{10,... | collective-permute-start | bytes 61448 | tf_op jit(solution)/shard_map/while/body/eval_jaxpr/ppermute | solution.py:64
  6.7 6.7 %collective-permute-start.2 = (bf16[1,5,2048]{2,1,0:T(8,128)(2,1)S(1)}, bf16[1,5,2048]{2,1,0:T(8,128)(2,1)S(1)}, u32[]{:S(2)}, u32[]{:S(2)}) collective-permute-start(bf16[1,5,2048]{2,1,0:T(8,128)(2,1)S(1)} %get-tuple-element.761), channel_id=1, source_target_pairs={{0,3},{1,2},{2,1},{3,0},{4,7},{5,6},{6,5},{7,4},{8,11},{9,10},{10,... | collective-permute-start | bytes 61448 | tf_op jit(solution)/shard_map/while/body/eval_jaxpr/ppermute | solution.py:64
  19.1 13.1 %all-to-all-start = ((bf16[8,5,2048]{2,1,0:T(8,128)(2,1)}), bf16[8,5,2048]{2,1,0:T(8,128)(2,1)S(1)}, u32[]{:S(2)}, u32[]{:S(2)}) async-start(bf16[8,5,2048]{2,1,0:T(8,128)(2,1)} %get-tuple-element.857), calls=%async_computation | async-start | bytes 524288 | tf_op jit(solution)/shard_map/while/body/eval_jaxpr/all_to_all | solution.py:69
  33.5 6.5 %collective-permute-start.7 = (bf16[3,8,2048]{2,1,0:T(8,128)(2,1)S(1)}, bf16[3,8,2048]{2,1,0:T(8,128)(2,1)S(1)}, u32[]{:S(2)}, u32[]{:S(2)}) collective-permute-start(bf16[3,8,2048]{2,1,0:T(8,128)(2,1)S(1)} %maximum_select_fusion.2), channel_id=1, source_target_pairs={{0,8},{8,16},{16,24},{1,9},{9,17},{17,25},{2,10},{10,18},{18,26},{... | collective-permute-start | bytes 294920 | tf_op jit(solution)/shard_map/while/body/eval_jaxpr/ppermute | solution.py:16
  42.9 8.0 %collective-permute-start.2 = (bf16[1,5,2048]{2,1,0:T(8,128)(2,1)S(1)}, bf16[1,5,2048]{2,1,0:T(8,128)(2,1)S(1)}, u32[]{:S(2)}, u32[]{:S(2)}) collective-permute-start(bf16[1,5,2048]{2,1,0:T(8,128)(2,1)S(1)} %get-tuple-element.761), channel_id=1, source_target_pairs={{0,3},{1,2},{2,1},{3,0},{4,7},{5,6},{6,5},{7,4},{8,11},{9,10},{10,... | collective-permute-start | bytes 61448 | tf_op jit(solution)/shard_map/while/body/eval_jaxpr/ppermute | solution.py:64
  54.6 13.4 %all-to-all-start = ((bf16[8,5,2048]{2,1,0:T(8,128)(2,1)}), bf16[8,5,2048]{2,1,0:T(8,128)(2,1)S(1)}, u32[]{:S(2)}, u32[]{:S(2)}) async-start(bf16[8,5,2048]{2,1,0:T(8,128)(2,1)} %get-tuple-element.857), calls=%async_computation | async-start | bytes 524288 | tf_op jit(solution)/shard_map/while/body/eval_jaxpr/all_to_all | solution.py:69
  78.7 8.0 %collective-permute-start.2 = (bf16[1,5,2048]{2,1,0:T(8,128)(2,1)S(1)}, bf16[1,5,2048]{2,1,0:T(8,128)(2,1)S(1)}, u32[]{:S(2)}, u32[]{:S(2)}) collective-permute-start(bf16[1,5,2048]{2,1,0:T(8,128)(2,1)S(1)} %get-tuple-element.761), channel_id=1, source_target_pairs={{0,3},{1,2},{2,1},{3,0},{4,7},{5,6},{6,5},{7,4},{8,11},{9,10},{10,... | collective-permute-start | bytes 61448 | tf_op jit(solution)/shard_map/while/body/eval_jaxpr/ppermute | solution.py:64
  90.5 13.4 %all-to-all-start = ((bf16[8,5,2048]{2,1,0:T(8,128)(2,1)}), bf16[8,5,2048]{2,1,0:T(8,128)(2,1)S(1)}, u32[]{:S(2)}, u32[]{:S(2)}) async-start(bf16[8,5,2048]{2,1,0:T(8,128)(2,1)} %get-tuple-element.857), calls=%async_computation | async-start | bytes 524288 | tf_op jit(solution)/shard_map/while/body/eval_jaxpr/all_to_all | solution.py:69
  105.3 39.9 %collective-permute-start.7 = (bf16[3,8,2048]{2,1,0:T(8,128)(2,1)S(1)}, bf16[3,8,2048]{2,1,0:T(8,128)(2,1)S(1)}, u32[]{:S(2)}, u32[]{:S(2)}) collective-permute-start(bf16[3,8,2048]{2,1,0:T(8,128)(2,1)S(1)} %maximum_select_fusion.2), channel_id=1, source_target_pairs={{0,8},{8,16},{16,24},{1,9},{9,17},{17,25},{2,10},{10,18},{18,26},{... | collective-permute-start | bytes 294920 | tf_op jit(solution)/shard_map/while/body/eval_jaxpr/ppermute | solution.py:16
  148.1 8.0 %collective-permute-start.2 = (bf16[1,5,2048]{2,1,0:T(8,128)(2,1)S(1)}, bf16[1,5,2048]{2,1,0:T(8,128)(2,1)S(1)}, u32[]{:S(2)}, u32[]{:S(2)}) collective-permute-start(bf16[1,5,2048]{2,1,0:T(8,128)(2,1)S(1)} %get-tuple-element.761), channel_id=1, source_target_pairs={{0,3},{1,2},{2,1},{3,0},{4,7},{5,6},{6,5},{7,4},{8,11},{9,10},{10,... | collective-permute-start | bytes 61448 | tf_op jit(solution)/shard_map/while/body/eval_jaxpr/ppermute | solution.py:64
  172.6 13.1 %all-to-all-start = ((bf16[8,5,2048]{2,1,0:T(8,128)(2,1)}), bf16[8,5,2048]{2,1,0:T(8,128)(2,1)S(1)}, u32[]{:S(2)}, u32[]{:S(2)}) async-start(bf16[8,5,2048]{2,1,0:T(8,128)(2,1)} %get-tuple-element.857), calls=%async_computation | async-start | bytes 524288 | tf_op jit(solution)/shard_map/while/body/eval_jaxpr/all_to_all | solution.py:69
  187.1 7.4 %collective-permute-start.7 = (bf16[3,8,2048]{2,1,0:T(8,128)(2,1)S(1)}, bf16[3,8,2048]{2,1,0:T(8,128)(2,1)S(1)}, u32[]{:S(2)}, u32[]{:S(2)}) collective-permute-start(bf16[3,8,2048]{2,1,0:T(8,128)(2,1)S(1)} %maximum_select_fusion.2), channel_id=1, source_target_pairs={{0,8},{8,16},{16,24},{1,9},{9,17},{17,25},{2,10},{10,18},{18,26},{... | collective-permute-start | bytes 294920 | tf_op jit(solution)/shard_map/while/body/eval_jaxpr/ppermute | solution.py:16
  197.4 8.0 %collective-permute-start.2 = (bf16[1,5,2048]{2,1,0:T(8,128)(2,1)S(1)}, bf16[1,5,2048]{2,1,0:T(8,128)(2,1)S(1)}, u32[]{:S(2)}, u32[]{:S(2)}) collective-permute-start(bf16[1,5,2048]{2,1,0:T(8,128)(2,1)S(1)} %get-tuple-element.761), channel_id=1, source_target_pairs={{0,3},{1,2},{2,1},{3,0},{4,7},{5,6},{6,5},{7,4},{8,11},{9,10},{10,... | collective-permute-start | bytes 61448 | tf_op jit(solution)/shard_map/while/body/eval_jaxpr/ppermute | solution.py:64
  221.9 13.1 %all-to-all-start = ((bf16[8,5,2048]{2,1,0:T(8,128)(2,1)}), bf16[8,5,2048]{2,1,0:T(8,128)(2,1)S(1)}, u32[]{:S(2)}, u32[]{:S(2)}) async-start(bf16[8,5,2048]{2,1,0:T(8,128)(2,1)} %get-tuple-element.857), calls=%async_computation | async-start | bytes 524288 | tf_op jit(solution)/shard_map/while/body/eval_jaxpr/all_to_all | solution.py:69
  236.4 7.4 %collective-permute-start.7 = (bf16[3,8,2048]{2,1,0:T(8,128)(2,1)S(1)}, bf16[3,8,2048]{2,1,0:T(8,128)(2,1)S(1)}, u32[]{:S(2)}, u32[]{:S(2)}) collective-permute-start(bf16[3,8,2048]{2,1,0:T(8,128)(2,1)S(1)} %maximum_select_fusion.2), channel_id=1, source_target_pairs={{0,8},{8,16},{16,24},{1,9},{9,17},{17,25},{2,10},{10,18},{18,26},{... | collective-permute-start | bytes 294920 | tf_op jit(solution)/shard_map/while/body/eval_jaxpr/ppermute | solution.py:16
  246.7 8.0 %collective-permute-start.2 = (bf16[1,5,2048]{2,1,0:T(8,128)(2,1)S(1)}, bf16[1,5,2048]{2,1,0:T(8,128)(2,1)S(1)}, u32[]{:S(2)}, u32[]{:S(2)}) collective-permute-start(bf16[1,5,2048]{2,1,0:T(8,128)(2,1)S(1)} %get-tuple-element.761), channel_id=1, source_target_pairs={{0,3},{1,2},{2,1},{3,0},{4,7},{5,6},{6,5},{7,4},{8,11},{9,10},{10,... | collective-permute-start | bytes 61448 | tf_op jit(solution)/shard_map/while/body/eval_jaxpr/ppermute | solution.py:64
  271.2 13.1 %all-to-all-start = ((bf16[8,5,2048]{2,1,0:T(8,128)(2,1)}), bf16[8,5,2048]{2,1,0:T(8,128)(2,1)S(1)}, u32[]{:S(2)}, u32[]{:S(2)}) async-start(bf16[8,5,2048]{2,1,0:T(8,128)(2,1)} %get-tuple-element.857), calls=%async_computation | async-start | bytes 524288 | tf_op jit(solution)/shard_map/while/body/eval_jaxpr/all_to_all | solution.py:69
  285.7 7.4 %collective-permute-start.7 = (bf16[3,8,2048]{2,1,0:T(8,128)(2,1)S(1)}, bf16[3,8,2048]{2,1,0:T(8,128)(2,1)S(1)}, u32[]{:S(2)}, u32[]{:S(2)}) collective-permute-start(bf16[3,8,2048]{2,1,0:T(8,128)(2,1)S(1)} %maximum_select_fusion.2), channel_id=1, source_target_pairs={{0,8},{8,16},{16,24},{1,9},{9,17},{17,25},{2,10},{10,18},{18,26},{... | collective-permute-start | bytes 294920 | tf_op jit(solution)/shard_map/while/body/eval_jaxpr/ppermute | solution.py:16
  296.0 8.0 %collective-permute-start.2 = (bf16[1,5,2048]{2,1,0:T(8,128)(2,1)S(1)}, bf16[1,5,2048]{2,1,0:T(8,128)(2,1)S(1)}, u32[]{:S(2)}, u32[]{:S(2)}) collective-permute-start(bf16[1,5,2048]{2,1,0:T(8,128)(2,1)S(1)} %get-tuple-element.761), channel_id=1, source_target_pairs={{0,3},{1,2},{2,1},{3,0},{4,7},{5,6},{6,5},{7,4},{8,11},{9,10},{10,... | collective-permute-start | bytes 61448 | tf_op jit(solution)/shard_map/while/body/eval_jaxpr/ppermute | solution.py:64
  320.5 13.1 %all-to-all-start = ((bf16[8,5,2048]{2,1,0:T(8,128)(2,1)}), bf16[8,5,2048]{2,1,0:T(8,128)(2,1)S(1)}, u32[]{:S(2)}, u32[]{:S(2)}) async-start(bf16[8,5,2048]{2,1,0:T(8,128)(2,1)} %get-tuple-element.857), calls=%async_computation | async-start | bytes 524288 | tf_op jit(solution)/shard_map/while/body/eval_jaxpr/all_to_all | solution.py:69
  335.0 7.4 %collective-permute-start.7 = (bf16[3,8,2048]{2,1,0:T(8,128)(2,1)S(1)}, bf16[3,8,2048]{2,1,0:T(8,128)(2,1)S(1)}, u32[]{:S(2)}, u32[]{:S(2)}) collective-permute-start(bf16[3,8,2048]{2,1,0:T(8,128)(2,1)S(1)} %maximum_select_fusion.2), channel_id=1, source_target_pairs={{0,8},{8,16},{16,24},{1,9},{9,17},{17,25},{2,10},{10,18},{18,26},{... | collective-permute-start | bytes 294920 | tf_op jit(solution)/shard_map/while/body/eval_jaxpr/ppermute | solution.py:16
  345.3 8.0 %collective-permute-start.2 = (bf16[1,5,2048]{2,1,0:T(8,128)(2,1)S(1)}, bf16[1,5,2048]{2,1,0:T(8,128)(2,1)S(1)}, u32[]{:S(2)}, u32[]{:S(2)}) collective-permute-start(bf16[1,5,2048]{2,1,0:T(8,128)(2,1)S(1)} %get-tuple-element.761), channel_id=1, source_target_pairs={{0,3},{1,2},{2,1},{3,0},{4,7},{5,6},{6,5},{7,4},{8,11},{9,10},{10,... | collective-permute-start | bytes 61448 | tf_op jit(solution)/shard_map/while/body/eval_jaxpr/ppermute | solution.py:64
  369.9 13.1 %all-to-all-start = ((bf16[8,5,2048]{2,1,0:T(8,128)(2,1)}), bf16[8,5,2048]{2,1,0:T(8,128)(2,1)S(1)}, u32[]{:S(2)}, u32[]{:S(2)}) async-start(bf16[8,5,2048]{2,1,0:T(8,128)(2,1)} %get-tuple-element.857), calls=%async_computation | async-start | bytes 524288 | tf_op jit(solution)/shard_map/while/body/eval_jaxpr/all_to_all | solution.py:69
  384.3 7.4 %collective-permute-start.7 = (bf16[3,8,2048]{2,1,0:T(8,128)(2,1)S(1)}, bf16[3,8,2048]{2,1,0:T(8,128)(2,1)S(1)}, u32[]{:S(2)}, u32[]{:S(2)}) collective-permute-start(bf16[3,8,2048]{2,1,0:T(8,128)(2,1)S(1)} %maximum_select_fusion.2), channel_id=1, source_target_pairs={{0,8},{8,16},{16,24},{1,9},{9,17},{17,25},{2,10},{10,18},{18,26},{... | collective-permute-start | bytes 294920 | tf_op jit(solution)/shard_map/while/body/eval_jaxpr/ppermute | solution.py:16
  394.6 8.0 %collective-permute-start.2 = (bf16[1,5,2048]{2,1,0:T(8,128)(2,1)S(1)}, bf16[1,5,2048]{2,1,0:T(8,128)(2,1)S(1)}, u32[]{:S(2)}, u32[]{:S(2)}) collective-permute-start(bf16[1,5,2048]{2,1,0:T(8,128)(2,1)S(1)} %get-tuple-element.761), channel_id=1, source_target_pairs={{0,3},{1,2},{2,1},{3,0},{4,7},{5,6},{6,5},{7,4},{8,11},{9,10},{10,... | collective-permute-start | bytes 61448 | tf_op jit(solution)/shard_map/while/body/eval_jaxpr/ppermute | solution.py:64
  419.2 13.1 %all-to-all-start = ((bf16[8,5,2048]{2,1,0:T(8,128)(2,1)}), bf16[8,5,2048]{2,1,0:T(8,128)(2,1)S(1)}, u32[]{:S(2)}, u32[]{:S(2)}) async-start(bf16[8,5,2048]{2,1,0:T(8,128)(2,1)} %get-tuple-element.857), calls=%async_computation | async-start | bytes 524288 | tf_op jit(solution)/shard_map/while/body/eval_jaxpr/all_to_all | solution.py:69
  433.7 7.4 %collective-permute-start.7 = (bf16[3,8,2048]{2,1,0:T(8,128)(2,1)S(1)}, bf16[3,8,2048]{2,1,0:T(8,128)(2,1)S(1)}, u32[]{:S(2)}, u32[]{:S(2)}) collective-permute-start(bf16[3,8,2048]{2,1,0:T(8,128)(2,1)S(1)} %maximum_select_fusion.2), channel_id=1, source_target_pairs={{0,8},{8,16},{16,24},{1,9},{9,17},{17,25},{2,10},{10,18},{18,26},{... | collective-permute-start | bytes 294920 | tf_op jit(solution)/shard_map/while/body/eval_jaxpr/ppermute | solution.py:16
  443.9 8.0 %collective-permute-start.2 = (bf16[1,5,2048]{2,1,0:T(8,128)(2,1)S(1)}, bf16[1,5,2048]{2,1,0:T(8,128)(2,1)S(1)}, u32[]{:S(2)}, u32[]{:S(2)}) collective-permute-start(bf16[1,5,2048]{2,1,0:T(8,128)(2,1)S(1)} %get-tuple-element.761), channel_id=1, source_target_pairs={{0,3},{1,2},{2,1},{3,0},{4,7},{5,6},{6,5},{7,4},{8,11},{9,10},{10,... | collective-permute-start | bytes 61448 | tf_op jit(solution)/shard_map/while/body/eval_jaxpr/ppermute | solution.py:64
  468.5 13.1 %all-to-all-start = ((bf16[8,5,2048]{2,1,0:T(8,128)(2,1)}), bf16[8,5,2048]{2,1,0:T(8,128)(2,1)S(1)}, u32[]{:S(2)}, u32[]{:S(2)}) async-start(bf16[8,5,2048]{2,1,0:T(8,128)(2,1)} %get-tuple-element.857), calls=%async_computation | async-start | bytes 524288 | tf_op jit(solution)/shard_map/while/body/eval_jaxpr/all_to_all | solution.py:69
  483.0 7.4 %collective-permute-start.7 = (bf16[3,8,2048]{2,1,0:T(8,128)(2,1)S(1)}, bf16[3,8,2048]{2,1,0:T(8,128)(2,1)S(1)}, u32[]{:S(2)}, u32[]{:S(2)}) collective-permute-start(bf16[3,8,2048]{2,1,0:T(8,128)(2,1)S(1)} %maximum_select_fusion.2), channel_id=1, source_target_pairs={{0,8},{8,16},{16,24},{1,9},{9,17},{17,25},{2,10},{10,18},{18,26},{... | collective-permute-start | bytes 294920 | tf_op jit(solution)/shard_map/while/body/eval_jaxpr/ppermute | solution.py:16
  493.2 8.0 %collective-permute-start.2 = (bf16[1,5,2048]{2,1,0:T(8,128)(2,1)S(1)}, bf16[1,5,2048]{2,1,0:T(8,128)(2,1)S(1)}, u32[]{:S(2)}, u32[]{:S(2)}) collective-permute-start(bf16[1,5,2048]{2,1,0:T(8,128)(2,1)S(1)} %get-tuple-element.761), channel_id=1, source_target_pairs={{0,3},{1,2},{2,1},{3,0},{4,7},{5,6},{6,5},{7,4},{8,11},{9,10},{10,... | collective-permute-start | bytes 61448 | tf_op jit(solution)/shard_map/while/body/eval_jaxpr/ppermute | solution.py:64
  517.8 13.1 %all-to-all-start = ((bf16[8,5,2048]{2,1,0:T(8,128)(2,1)}), bf16[8,5,2048]{2,1,0:T(8,128)(2,1)S(1)}, u32[]{:S(2)}, u32[]{:S(2)}) async-start(bf16[8,5,2048]{2,1,0:T(8,128)(2,1)} %get-tuple-element.857), calls=%async_computation | async-start | bytes 524288 | tf_op jit(solution)/shard_map/while/body/eval_jaxpr/all_to_all | solution.py:69
  (69 other events, 381.5 us)
